TPU v7x, 32 devices: a whole 2x2x4 slice. The times are simulated.
32 devices in a mesh: fsdp: 4 (over y, x), tp: 8 (over z, core).
Axes of the slice: x: 2, y: 2, z: 4, core: 2. Of those that a mesh axis runs over, the one named last changes fastest.
Arguments:
- ref_gate: bfloat16 [3072, 11008], P('fsdp', 'tp'), may hold values from -6 to 6
- ref_up: bfloat16 [3072, 11008], P('fsdp', 'tp'), may hold values from -6 to 6
- ref_residual: bfloat16 [3072, 4096], P('fsdp', 'tp'), may hold values from -6 to 6
- ref_modality: int32 [3072], P('fsdp'), may hold values 0 or 1
- ref_down_text: bfloat16 [4096, 11008], P('fsdp', 'tp'), may hold values from -0.0546875 to 0.0546875
- ref_down_image: bfloat16 [4096, 11008], P('fsdp', 'tp'), may hold values from -0.0546875 to 0.0546875
- pol_gate: bfloat16 [3072, 11008], P('fsdp', 'tp'), may hold values from -6 to 6
- pol_up: bfloat16 [3072, 11008], P('fsdp', 'tp'), may hold values from -6 to 6
- pol_modality: int32 [3072], P('fsdp'), may hold values 0 or 1
- pol_segment: int32 [3072], P('fsdp'), may hold values from 0 to 5, never falling along the last dimension, each value on 1 to 768 neighbouring positions
- pair_margin: float32 [3], replicated, may hold values from -30 to 30
- token_cotangent: bfloat16 [3072, 4096], P('fsdp', 'tp'), may hold values from -24 to 24
- pol_down_text: bfloat16 [4096, 11008], P('fsdp', 'tp'), may hold values from -0.0546875 to 0.0546875
- pol_down_image: bfloat16 [4096, 11008], P('fsdp', 'tp'), may hold values from -0.0546875 to 0.0546875
Outputs:
- ref_out: bfloat16 [3072, 4096], P('fsdp', 'tp')
- grad_gate: bfloat16 [3072, 11008], P('fsdp', 'tp')
- grad_up: bfloat16 [3072, 11008], P('fsdp', 'tp')
- grad_down_text: float32 [4096, 11008], P('fsdp', 'tp')
- grad_down_image: float32 [4096, 11008], P('fsdp', 'tp')
Inputs may be any that keep to these rules, and one draw needn't show every extreme that they name: `ref_modality`: 0 marks a text token, 1 an image token. `pol_modality`: 0 marks a text token, 1 an image token. `pol_segment`: response numbers never fall along the tokens; responses 2p and 2p + 1 are the chosen and the rejected response of pair p; every response has at least one token.
All inputs are finite; a program needn't handle non-finite values. No bound on the sum of `ref_modality` or of `pol_modality` on one device may be relied on, other than what follows from the above.
Results may differ from a plain program's by a relative error of at most 0.015.
Values may be sent and summed in bfloat16 or wider, within the bound.
A program may use at most 192 MiB of HBM per device.

v0:
```python
import jax
import jax.numpy as jnp
from jax import lax
from jax.sharding import PartitionSpec as P

dpo_beta = 0.1


def split_hidden(gate, up, modality):
    gate_f = gate.astype(jnp.float32)
    up_f = up.astype(jnp.float32)
    sig = jax.nn.sigmoid(gate_f)
    act = gate_f * sig
    hidden = (act * up_f).astype(jnp.bfloat16)
    image = (modality == 1)[:, None]
    zero = jnp.zeros_like(hidden)
    return (jnp.where(image, zero, hidden), jnp.where(image, hidden, zero), gate_f, up_f, sig, act)


def forward_term(left_text, left_image, right_text, right_image):
    contract = (((1,), (1,)), ((), ()))
    part = lax.dot_general(left_text, right_text, contract, preferred_element_type=jnp.float32)
    return part + lax.dot_general(
        left_image, right_image, contract, preferred_element_type=jnp.float32
    )


def backward_term(left_text, left_image, right_text, right_image):
    part = jnp.dot(left_text, right_text, preferred_element_type=jnp.float32)
    return part + jnp.dot(left_image, right_image, preferred_element_type=jnp.float32)


def per_device(
    ref_gate,
    ref_up,
    ref_residual,
    ref_modality,
    ref_down_text,
    ref_down_image,
    pol_gate,
    pol_up,
    pol_modality,
    pol_segment,
    pair_margin,
    token_cotangent,
    pol_down_text,
    pol_down_image,
):
    ref_text, ref_image, _, _, _, _ = split_hidden(ref_gate, ref_up, ref_modality)
    pol_text, pol_image, gate_f, up_f, sig, act = split_hidden(pol_gate, pol_up, pol_modality)
    seg_ids = jnp.arange(2 * pair_margin.shape[0], dtype=jnp.int32)
    pair_weight = dpo_beta * jax.nn.sigmoid(-dpo_beta * pair_margin)
    table = jnp.repeat(pair_weight, 2) * jnp.where(seg_ids % 2 == 0, -1.0, 1.0).astype(jnp.float32)
    coef = jnp.sum(
        jnp.where(pol_segment[:, None] == seg_ids[None, :], table[None, :], jnp.float32(0.0)),
        axis=1,
    )
    local_cot = (coef[:, None] * token_cotangent.astype(jnp.float32)).astype(jnp.bfloat16)
    full_cot = lax.all_gather(local_cot, "tp", axis=1, tiled=True)
    image_p = (pol_modality == 1)[:, None]
    zero_cot = jnp.zeros_like(full_cot)
    cot_text = jnp.where(image_p, zero_cot, full_cot)
    cot_image = jnp.where(image_p, full_cot, zero_cot)
    stacked_ref = jnp.stack([ref_down_text, ref_down_image])
    piece = lax.all_gather(stacked_ref, "fsdp", axis=1, tiled=True)
    terms = forward_term(ref_text, ref_image, piece[0], piece[1])
    d_hidden = backward_term(
        cot_text,
        cot_image,
        lax.all_gather(pol_down_text, "fsdp", axis=0, tiled=True),
        lax.all_gather(pol_down_image, "fsdp", axis=0, tiled=True),
    )
    summed = lax.psum_scatter(
        terms.astype(jnp.bfloat16), "tp", scatter_dimension=1, tiled=True
    ).astype(jnp.float32)
    ref_out = (summed + ref_residual.astype(jnp.float32)).astype(jnp.bfloat16)
    grad_gate = (d_hidden * up_f * sig * (1.0 + gate_f * (1.0 - sig))).astype(jnp.bfloat16)
    grad_up = (d_hidden * act).astype(jnp.bfloat16)
    width = pol_down_text.shape[1]
    over_rows = (((0,), (0,)), ((), ()))
    term_text = lax.dot_general(cot_text, pol_text, over_rows, preferred_element_type=jnp.float32)
    term_image = lax.dot_general(
        cot_image, pol_image, over_rows, preferred_element_type=jnp.float32
    )
    grads = lax.psum_scatter(
        jnp.concatenate([term_text, term_image], axis=1).astype(jnp.bfloat16),
        "fsdp",
        scatter_dimension=0,
        tiled=True,
    ).astype(jnp.float32)
    return (ref_out, grad_gate, grad_up, grads[:, :width], grads[:, width:])


def solution(mesh):
    in_specs = (
        P("fsdp", "tp"),
        P("fsdp", "tp"),
        P("fsdp", "tp"),
        P("fsdp"),
        P("fsdp", "tp"),
        P("fsdp", "tp"),
        P("fsdp", "tp"),
        P("fsdp", "tp"),
        P("fsdp"),
        P("fsdp"),
        P(),
        P("fsdp", "tp"),
        P("fsdp", "tp"),
        P("fsdp", "tp"),
    )
    out_specs = (
        P("fsdp", "tp"),
        P("fsdp", "tp"),
        P("fsdp", "tp"),
        P("fsdp", "tp"),
        P("fsdp", "tp"),
    )
    return jax.shard_map(
        per_device, mesh=mesh, in_specs=in_specs, out_specs=out_specs, check_vma=False
    )
```

profile of v0, /device:TPU:0, one launch (start us, length us, event | category | flops | bytes accessed | tf_op | source)
XLA Modules:
  0.0 803.0 jit_solution(6594723527638454698)
XLA Ops:
  7.2 5.7 pad_maximum_fusion.1
  13.0 0.6 copy-done.10
  13.6 0.1 reshape.33
  13.8 0.2 copy-done
  14.0 1.1 multiply_convert_fusion.1
  15.2 0.7 all-gather.9.cloned.1.call-update
  15.9 0.5 all-gather.11.cloned.1.call-update
  16.5 205.2 %all-gather.5.cloned.1.call-done = bf16[2,4096,1376]{1,2,0:T(8,128)(2,1)} async-done(((bf16[2,1024,1376]{1,2,0:T(8,128)(2,1)}), bf16[2,4096,1376]{1,2,0:T(8,128)(2,1)}) %all-gather.5.cloned.1.call-update) | async-done | bytes 22544400 | tf_op jit(solution)/shard_map/all_gather | solution.py:65
  221.8 18.6 %fusion = f32[768,4096]{1,0:T(8,128)} fusion(bf16[2,4096,1376]{1,2,0:T(8,128)(2,1)} %all-gather.5.cloned.1.call-done, pred[768]{0:T(1024)(128)(4,1)S(1)} %broadcast_compare_fusion.1, bf16[768,1376]{0,1:T(8,128)(2,1)S(1)} %copy-done.6, bf16[768,1376]{0,1:T(8,128)(2,1)} %param.14), kind=kOutput, calls=%fused_computation.5 | convolution fusion | flops 8666554368 | bytes 28082944 | tf_op jit(solution)/shard_map/dot_general | solution.py:23
  240.3 18.3 %add_convert_fusion = bf16[768,4096]{1,0:T(8,128)(2,1)} fusion(f32[768,4096]{1,0:T(8,128)} %fusion, bf16[2,4096,1376]{1,2,0:T(8,128)(2,1)} %all-gather.5.cloned.1.call-done, pred[768]{0:T(1024)(128)(4,1)S(1)} %broadcast_compare_fusion.1, bf16[768,1376]{0,1:T(8,128)(2,1)S(1)} %copy-done.6, bf16[768,1376]{0,1:T(8,128)(2,1)S(1)} %copy-done.7), kind=kOutput, calls=%fused_computation.3 | convolution fusion | flops 8672845824 | bytes 34374400 | tf_op jit(solution)/shard_map/dot_general | solution.py:22
  258.7 0.2 reduce-scatter.5.cloned.1.call-start
  258.9 0.4 copy-done.3
  259.4 29.3 %all-gather.7.cloned.1.call-done = bf16[768,4096]{1,0:T(8,128)(2,1)} async-done(((bf16[768,512]{1,0:T(8,128)(2,1)}), bf16[768,4096]{1,0:T(8,128)(2,1)}) %all-gather.7.cloned.1.call-update) | async-done | bytes 6291472 | tf_op jit(solution)/shard_map/all_gather | solution.py:59
  288.7 15.3 %convolution_convert_fusion = bf16[4096,1376]{0,1:T(8,128)(2,1)} fusion(bf16[768,4096]{1,0:T(8,128)(2,1)} %all-gather.7.cloned.1.call-done, pred[768]{0:T(1024)(128)(4,1)S(1)} %broadcast_compare_fusion, bf16[768,1376]{0,1:T(8,128)(2,1)} %param.21, bf16[768,1376]{0,1:T(8,128)(2,1)S(1)} %copy-done.8), kind=kOutput, calls=%fused_computation.1 | convolution fusion | flops 8675336192 | bytes 21791488 | tf_op jit(solution)/shard_map/dot_general | solution.py:82
  304.0 12.3 %convolution_convert_fusion.1 = bf16[4096,1376]{0,1:T(8,128)(2,1)} fusion(bf16[768,4096]{1,0:T(8,128)(2,1)S(1)} %copy-done.5, pred[768]{0:T(1024)(128)(4,1)S(1)} %broadcast_compare_fusion, bf16[768,1376]{0,1:T(8,128)(2,1)S(1)} %copy-done.9, bf16[768,1376]{0,1:T(8,128)(2,1)S(1)} %copy-done.8), kind=kOutput, calls=%fused_computation.2 | convolution fusion | flops 8675336192 | bytes 21791488 | tf_op jit(solution)/shard_map/dot_general | solution.py:81
  316.3 20.2 %pad_maximum_fusion = bf16[4096,2752]{0,1:T(8,128)(2,1)} fusion(bf16[4096,1376]{0,1:T(8,128)(2,1)} %convolution_convert_fusion, bf16[4096,1376]{0,1:T(8,128)(2,1)} %convolution_convert_fusion.1), kind=kLoop, calls=%fused_computation | loop fusion | flops 45088768 | bytes 45088768 | tf_op jit(solution)/shard_map/concatenate | solution.py:86
  336.4 64.2 %all-gather.9.cloned.1.call-done = bf16[4096,1376]{0,1:T(8,128)(2,1)} async-done(((bf16[1024,1376]{0,1:T(8,128)(2,1)}), bf16[4096,1376]{0,1:T(8,128)(2,1)}) %all-gather.9.cloned.1.call-update) | async-done | bytes 11272208 | tf_op jit(solution)/shard_map/all_gather | solution.py:70
  400.7 15.1 %fusion.15 = f32[768,1376]{0,1:T(8,128)} fusion(bf16[4096,1376]{0,1:T(8,128)(2,1)} %all-gather.9.cloned.1.call-done, bf16[768,4096]{1,0:T(8,128)(2,1)} %all-gather.7.cloned.1.call-done, pred[768]{0:T(1024)(128)(4,1)S(1)} %broadcast_compare_fusion), kind=kOutput, calls=%fused_computation.33 | convolution fusion | flops 8660189184 | bytes 21791488 | tf_op jit(solution)/shard_map/dot_general | solution.py:29
  415.8 98.1 %all-gather.11.cloned.1.call-done = bf16[4096,1376]{0,1:T(8,128)(2,1)} async-done(((bf16[1024,1376]{0,1:T(8,128)(2,1)}), bf16[4096,1376]{0,1:T(8,128)(2,1)}) %all-gather.11.cloned.1.call-update) | async-done | bytes 11272208 | tf_op jit(solution)/shard_map/all_gather | solution.py:71
  513.9 17.5 %multiply_convert_fusion = (bf16[768,1376]{0,1:T(8,128)(2,1)}, bf16[768,1376]{0,1:T(8,128)(2,1)}) fusion(bf16[768,1376]{0,1:T(8,128)(2,1)S(1)} %copy-done.8, bf16[768,1376]{0,1:T(8,128)(2,1)} %param.21, f32[768,1376]{0,1:T(8,128)} %fusion.15, bf16[4096,1376]{0,1:T(8,128)(2,1)} %all-gather.11.cloned.1.call-done, ...), kind=kOutput, calls=%fused_computation.30 | convolution fusion | flops 8677097472 | bytes 30245632 | tf_op jit(solution)/shard_map/dot_general | solution.py:30
  531.4 54.4 %reduce-scatter.3.cloned.1.call-done = bf16[768,512]{1,0:T(8,128)(2,1)} async-done(((bf16[768,4096]{1,0:T(8,128)(2,1)}), bf16[768,512]{1,0:T(8,128)(2,1)}) %reduce-scatter.3.cloned.1.call-update) | async-done | bytes 786448 | tf_op jit(solution)/shard_map/reduce_scatter | solution.py:73
  585.8 2.2 add_convert_fusion.1
  588.0 199.8 %reduce-scatter.5.cloned.1.call-done = bf16[1024,2752]{0,1:T(8,128)(2,1)} async-done(((bf16[4096,2752]{0,1:T(8,128)(2,1)}), bf16[1024,2752]{0,1:T(8,128)(2,1)}) %reduce-scatter.5.cloned.1.call-update) | async-done | bytes 5636112 | tf_op jit(solution)/shard_map/reduce_scatter | solution.py:85
  787.8 8.3 %fusion.39 = (f32[1024,1376]{0,1:T(8,128)}, f32[1024,1376]{0,1:T(8,128)}) fusion(bf16[1024,2752]{0,1:T(8,128)(2,1)} %reduce-scatter.5.cloned.1.call-done), kind=kLoop, calls=%fused_computation.62 | loop fusion | bytes 22544384 | tf_op jit(solution)/shard_map/slice | solution.py:91
  (34 shorter events, 0.5 us)
Async XLA Ops:
  7.2 214.6 %all-gather.5.cloned.1.call-start = ((), (), s32[]{:S(2)}) async-start(), calls=%async_computation.2 | async-start | bytes 28180480 | tf_op jit(solution)/shard_map/all_gather | solution.py:65
  12.9 0.7 copy-start.10
  12.9 0.8 copy-start.4
  12.9 1.2 copy-start
  12.9 3.6 copy-start.2
  12.9 208.9 %copy-start.6 = (bf16[768,1376]{0,1:T(8,128)(2,1)S(1)}, bf16[768,1376]{0,1:T(8,128)(2,1)}, u32[]{:S(2)}) copy-start(bf16[768,1376]{0,1:T(8,128)(2,1)} %param.15) | copy-start | bytes 6340612
  12.9 275.8 %all-gather.7.cloned.1.call-start = ((), (), s32[]{:S(2)}) async-start(), calls=%async_computation.4 | async-start | bytes 7077888 | tf_op jit(solution)/shard_map/all_gather | solution.py:59
  15.2 385.5 %all-gather.9.cloned.1.call-start = ((), (), s32[]{:S(2)}) async-start(), calls=%async_computation.5 | async-start | bytes 14090240 | tf_op jit(solution)/shard_map/all_gather | solution.py:70
  15.9 498.0 %all-gather.11.cloned.1.call-start = ((), (), s32[]{:S(2)}) async-start(), calls=%async_computation.6 | async-start | bytes 14090240 | tf_op jit(solution)/shard_map/all_gather | solution.py:71
  16.5 569.3 %reduce-scatter.3.cloned.1.call-start = ((), (), s32[]{:S(2)}) async-start(), calls=%async_computation.3 | async-start | bytes 7077888 | tf_op jit(solution)/shard_map/reduce_scatter | solution.py:73
  221.8 18.6 %copy-start.7 = (bf16[768,1376]{0,1:T(8,128)(2,1)S(1)}, bf16[768,1376]{0,1:T(8,128)(2,1)}, u32[]{:S(2)}) copy-start(bf16[768,1376]{0,1:T(8,128)(2,1)} %param.14) | copy-start | bytes 6340612
  258.7 0.7 copy-start.3
  258.7 30.0 %copy-start.8 = (bf16[768,1376]{0,1:T(8,128)(2,1)S(1)}, bf16[768,1376]{0,1:T(8,128)(2,1)}, u32[]{:S(2)}) copy-start(bf16[768,1376]{0,1:T(8,128)(2,1)} %param.20) | copy-start | bytes 6340612
  258.7 529.1 %reduce-scatter.5.cloned.1.call-start = ((), (), s32[]{:S(2)}) async-start(), calls=%async_computation.7 | async-start | bytes 28180480 | tf_op jit(solution)/shard_map/reduce_scatter | solution.py:85
  288.7 15.3 %copy-start.5 = (bf16[768,4096]{1,0:T(8,128)(2,1)S(1)}, bf16[768,4096]{1,0:T(8,128)(2,1)}, u32[]{:S(2)}) copy-start(bf16[768,4096]{1,0:T(8,128)(2,1)} %all-gather.7.cloned.1.call-done) | copy-start | bytes 18874372
  288.7 15.3 %copy-start.9 = (bf16[768,1376]{0,1:T(8,128)(2,1)S(1)}, bf16[768,1376]{0,1:T(8,128)(2,1)}, u32[]{:S(2)}) copy-start(bf16[768,1376]{0,1:T(8,128)(2,1)} %param.21) | copy-start | bytes 6340612
  415.8 170.1 %copy-start.1 = (bf16[768,512]{1,0:T(8,128)(2,1)S(1)}, bf16[768,512]{1,0:T(8,128)(2,1)}, u32[]{:S(2)}) copy-start(bf16[768,512]{1,0:T(8,128)(2,1)} %param.16) | copy-start | bytes 2359300
Sparse Core Ops, SparseCore 0:
  13.0 208.7 all-gather.4
  224.0 64.6 all-gather.6
  290.5 110.1 all-gather.8
  402.4 111.4 all-gather.10
  516.0 69.7 reduce-scatter.2
  588.8 198.9 reduce-scatter.4
where the time goes:
time: 803 us
  waiting for transfers between devices  652 us (81%)
  matrix products  97 us (12%)
  other arithmetic  29.2 us (4%)
  between operations  14.2 us (2%)
  local copies, waits for them, and re-layouts  9.76 us (1%)
    all_gather x1, waiting for transfers between devices, per_device(): piece = lax.all_gather(stacked_ref, 'fsdp', axis=1, tiled=True)  205 us
    reduce_scatter x1, waiting for transfers between devices, per_device(): lax.psum_scatter(jnp.concatenate([term_text, term_image], axis=1).astype(...  200 us
    all_gather x1, waiting for transfers between devices, per_device(): lax.all_gather(pol_down_image, 'fsdp', axis=0, tiled=True)  98.1 us
    all_gather x1, waiting for transfers between devices, per_device(): lax.all_gather(pol_down_text, 'fsdp', axis=0, tiled=True)  64.2 us
    reduce_scatter x1, waiting for transfers between devices, per_device(): lax.psum_scatter(terms.astype(jnp.bfloat16), 'tp', scatter_dimension=1, t...  54.4 us
    all_gather x1, waiting for transfers between devices, per_device(): full_cot = lax.all_gather(local_cot, 'tp', axis=1, tiled=True)  29.3 us
    concatenate x1, other arithmetic, per_device(): jnp.concatenate([term_text, term_image], axis=1).astype(jnp.bfloat16)  20.2 us
    dot_general x1, matrix products, forward_term(): lax.dot_general(left_image, right_image, contract, preferred_element_type...  18.6 us
  transfers between devices with their start and end apart: 6, of which 6 were waited for; matrix products, arithmetic and copies ran while one was open for 15% of the time, Pallas kernels for 0%

commit v1 on v0

--- a/solution.py
+++ b/solution.py
@@ -62,7 +62,7 @@
     cot_text = jnp.where(image_p, zero_cot, full_cot)
     cot_image = jnp.where(image_p, full_cot, zero_cot)
     stacked_ref = jnp.stack([ref_down_text, ref_down_image])
-    piece = lax.all_gather(stacked_ref, "fsdp", axis=1, tiled=True)
+    piece = jnp.concatenate(lax.all_gather(stacked_ref, "fsdp"), axis=1)
     terms = forward_term(ref_text, ref_image, piece[0], piece[1])
     d_hidden = backward_term(
         cot_text,

time: 803 us -> 804 us (level)
  local copies, waits for them, and re-layouts: 9.76 us -> 53.3 us
  waiting for transfers between devices: 652 us -> 612 us
    all_gather x1, waiting for transfers between devices: 29.3 us -> 0.01 us  [per_device(): full_cot = lax.all_gather(local_cot, 'tp', axis=1, tiled=True)]
    all_gather x0 -> x1, local copies, waits for them, and re-layouts: none -> 29.3 us  [per_device(): piece = jnp.concatenate(lax.all_gather(stacked_ref, 'fsdp'), axis=1)]
    slice x0 -> x1, local copies, waits for them, and re-layouts: none -> 12.8 us  [per_device(): terms = forward_term(ref_text, ref_image, piece[0], piece[1])]
    all_gather x1, waiting for transfers between devices: 64.2 us -> 53.4 us  [per_device(): lax.all_gather(pol_down_text, 'fsdp', axis=0, tiled=True)]
  transfers between devices with their start and end apart: 6 -> 6, of which waited for: 6 -> 5; matrix products, arithmetic and copies ran while one was open for 15% -> 20% of each run, Pallas kernels for 0% -> 0%
where the time goes in v1:
time: 804 us; the launch traced here: 803 us
  waiting for transfers between devices  612 us (76%)
  matrix products  93.7 us (12%)
  local copies, waits for them, and re-layouts  53.3 us (7%)
  other arithmetic  29.2 us (4%)
  between operations  14.2 us (2%)
    all_gather x1, waiting for transfers between devices, per_device(): piece = jnp.concatenate(lax.all_gather(stacked_ref, 'fsdp'), axis=1)  205 us
    reduce_scatter x1, waiting for transfers between devices, per_device(): lax.psum_scatter(jnp.concatenate([term_text, term_image], axis=1).astype(...  200 us
    all_gather x1, waiting for transfers between devices, per_device(): lax.all_gather(pol_down_image, 'fsdp', axis=0, tiled=True)  98.1 us
    reduce_scatter x1, waiting for transfers between devices, per_device(): lax.psum_scatter(terms.astype(jnp.bfloat16), 'tp', scatter_dimension=1, t...  54.4 us
    all_gather x1, waiting for transfers between devices, per_device(): lax.all_gather(pol_down_text, 'fsdp', axis=0, tiled=True)  53.4 us
    all_gather x1, local copies, waits for them, and re-layouts, per_device(): piece = jnp.concatenate(lax.all_gather(stacked_ref, 'fsdp'), axis=1)  29.3 us
    concatenate x1, other arithmetic, per_device(): jnp.concatenate([term_text, term_image], axis=1).astype(jnp.bfloat16)  20.1 us
    dot_general x1, matrix products, forward_term(): lax.dot_general(left_image, right_image, contract, preferred_element_type...  18.3 us
  transfers between devices with their start and end apart: 6, of which 5 were waited for; matrix products, arithmetic and copies ran while one was open for 20% of the time, Pallas kernels for 0%

profile of v1, /device:TPU:0, one launch (start us, length us, event | category | flops | bytes accessed | tf_op | source)
XLA Modules:
  0.0 803.0 jit_solution(17811932397686291448)
XLA Ops:
  7.2 5.7 pad_maximum_fusion.1
  13.0 0.6 copy-done.9
  13.8 0.2 copy-done
  14.0 1.1 multiply_convert_fusion.1
  15.2 0.7 all-gather.8.cloned.1.call-update
  15.9 0.5 all-gather.10.cloned.1.call-update
  16.5 205.2 %all-gather.12.cloned.1.call-done = bf16[8,1024,1376]{1,2,0:T(8,128)(2,1)} async-done(((bf16[2,1024,1376]{1,2,0:T(8,128)(2,1)}), bf16[8,1024,1376]{1,2,0:T(8,128)(2,1)}) %all-gather.12.cloned.1.call-update) | async-done | bytes 22544400 | tf_op jit(solution)/shard_map/all_gather | solution.py:65
  221.8 29.3 %copy.21 = bf16[4,2,1024,1376]{3,2,0,1:T(8,128)(2,1)} copy(bf16[4,2,1024,1376]{2,3,1,0:T(8,128)(2,1)} %bitcast.11) | data formatting | bytes 45088768 | tf_op jit(solution)/shard_map/all_gather | solution.py:65
  251.0 12.8 %fusion.38 = (bf16[1,4,1024,1376]{3,2,1,0:T(8,128)(2,1)}, bf16[1,4,1024,1376]{3,2,1,0:T(8,128)(2,1)S(1)}) fusion(bf16[2,4,1024,1376]{3,2,1,0:T(8,128)(2,1)} %bitcast.10), kind=kLoop, calls=%fused_computation.59 | loop fusion | bytes 45088768 | tf_op jit(solution)/shard_map/slice | solution.py:66
  263.8 14.2 %fusion.17 = f32[768,4096]{1,0:T(8,128)} fusion(bf16[4096,1376]{1,0:T(8,128)(2,1)S(1)} %bitcast.13, pred[768]{0:T(1024)(128)(4,1)S(1)} %broadcast_compare_fusion.1, bf16[768,1376]{0,1:T(8,128)(2,1)S(1)} %copy-done.6, bf16[768,1376]{0,1:T(8,128)(2,1)} %param.14), kind=kOutput, calls=%fused_computation.33 | convolution fusion | flops 8666554368 | bytes 28082944 | tf_op jit(solution)/shard_map/dot_general | solution.py:22
  278.0 18.3 %add_convert_fusion = bf16[768,4096]{1,0:T(8,128)(2,1)} fusion(f32[768,4096]{1,0:T(8,128)} %fusion.17, bf16[4096,1376]{1,0:T(8,128)(2,1)} %bitcast.12, pred[768]{0:T(1024)(128)(4,1)S(1)} %broadcast_compare_fusion.1, bf16[768,1376]{0,1:T(8,128)(2,1)S(1)} %copy-done.6, bf16[768,1376]{0,1:T(8,128)(2,1)} %param.14), kind=kOutput, calls=%fused_computation.3 | convolution fusion | flops 8672845824 | bytes 34374400 | tf_op jit(solution)/shard_map/dot_general | solution.py:23
  296.6 0.4 copy-done.3
  297.1 1.4 copy-done.7
  298.5 16.4 %convolution_convert_fusion = bf16[4096,1376]{0,1:T(8,128)(2,1)} fusion(bf16[768,4096]{1,0:T(8,128)(2,1)} %all-gather.6.cloned.1.call-done, pred[768]{0:T(1024)(128)(4,1)S(1)} %broadcast_compare_fusion, bf16[768,1376]{0,1:T(8,128)(2,1)} %param.21, bf16[768,1376]{0,1:T(8,128)(2,1)S(1)} %copy-done.7), kind=kOutput, calls=%fused_computation.1 | convolution fusion | flops 8675336192 | bytes 21791488 | tf_op jit(solution)/shard_map/dot_general | solution.py:82
  314.9 12.2 %convolution_convert_fusion.1 = bf16[4096,1376]{0,1:T(8,128)(2,1)} fusion(bf16[768,4096]{1,0:T(8,128)(2,1)S(1)} %copy-done.5, pred[768]{0:T(1024)(128)(4,1)S(1)} %broadcast_compare_fusion, bf16[768,1376]{0,1:T(8,128)(2,1)S(1)} %copy-done.8, bf16[768,1376]{0,1:T(8,128)(2,1)S(1)} %copy-done.7), kind=kOutput, calls=%fused_computation.2 | convolution fusion | flops 8675336192 | bytes 21791488 | tf_op jit(solution)/shard_map/dot_general | solution.py:81
  327.2 20.1 %pad_maximum_fusion = bf16[4096,2752]{0,1:T(8,128)(2,1)} fusion(bf16[4096,1376]{0,1:T(8,128)(2,1)} %convolution_convert_fusion, bf16[4096,1376]{0,1:T(8,128)(2,1)} %convolution_convert_fusion.1), kind=kLoop, calls=%fused_computation | loop fusion | flops 45088768 | bytes 45088768 | tf_op jit(solution)/shard_map/concatenate | solution.py:86
  347.3 53.4 %all-gather.8.cloned.1.call-done = bf16[4096,1376]{0,1:T(8,128)(2,1)} async-done(((bf16[1024,1376]{0,1:T(8,128)(2,1)}), bf16[4096,1376]{0,1:T(8,128)(2,1)}) %all-gather.8.cloned.1.call-update) | async-done | bytes 11272208 | tf_op jit(solution)/shard_map/all_gather | solution.py:70
  400.7 15.1 %fusion.13 = f32[768,1376]{0,1:T(8,128)} fusion(bf16[4096,1376]{0,1:T(8,128)(2,1)} %all-gather.8.cloned.1.call-done, bf16[768,4096]{1,0:T(8,128)(2,1)} %all-gather.6.cloned.1.call-done, pred[768]{0:T(1024)(128)(4,1)S(1)} %broadcast_compare_fusion), kind=kOutput, calls=%fused_computation.29 | convolution fusion | flops 8660189184 | bytes 21791488 | tf_op jit(solution)/shard_map/dot_general | solution.py:29
  415.8 98.1 %all-gather.10.cloned.1.call-done = bf16[4096,1376]{0,1:T(8,128)(2,1)} async-done(((bf16[1024,1376]{0,1:T(8,128)(2,1)}), bf16[4096,1376]{0,1:T(8,128)(2,1)}) %all-gather.10.cloned.1.call-update) | async-done | bytes 11272208 | tf_op jit(solution)/shard_map/all_gather | solution.py:71
  513.9 17.5 %multiply_convert_fusion = (bf16[768,1376]{0,1:T(8,128)(2,1)}, bf16[768,1376]{0,1:T(8,128)(2,1)}) fusion(bf16[768,1376]{0,1:T(8,128)(2,1)S(1)} %copy-done.7, bf16[768,1376]{0,1:T(8,128)(2,1)} %param.21, f32[768,1376]{0,1:T(8,128)} %fusion.13, bf16[4096,1376]{0,1:T(8,128)(2,1)} %all-gather.10.cloned.1.call-done, ...), kind=kOutput, calls=%fused_computation.26 | convolution fusion | flops 8677097472 | bytes 30245632 | tf_op jit(solution)/shard_map/dot_general | solution.py:30
  531.4 54.4 %reduce-scatter.3.cloned.1.call-done = bf16[768,512]{1,0:T(8,128)(2,1)} async-done(((bf16[768,4096]{1,0:T(8,128)(2,1)}), bf16[768,512]{1,0:T(8,128)(2,1)}) %reduce-scatter.3.cloned.1.call-update) | async-done | bytes 786448 | tf_op jit(solution)/shard_map/reduce_scatter | solution.py:73
  585.8 2.2 add_convert_fusion.1
  588.0 199.8 %reduce-scatter.5.cloned.1.call-done = bf16[1024,2752]{0,1:T(8,128)(2,1)} async-done(((bf16[4096,2752]{0,1:T(8,128)(2,1)}), bf16[1024,2752]{0,1:T(8,128)(2,1)}) %reduce-scatter.5.cloned.1.call-update) | async-done | bytes 5636112 | tf_op jit(solution)/shard_map/reduce_scatter | solution.py:85
  787.8 8.3 %fusion.39 = (f32[1024,1376]{0,1:T(8,128)}, f32[1024,1376]{0,1:T(8,128)}) fusion(bf16[1024,2752]{0,1:T(8,128)(2,1)} %reduce-scatter.5.cloned.1.call-done), kind=kLoop, calls=%fused_computation.60 | loop fusion | bytes 22544384 | tf_op jit(solution)/shard_map/slice | solution.py:91
  (34 shorter events, 0.8 us)
Async XLA Ops:
  7.2 214.6 %all-gather.12.cloned.1.call-start = ((), (), s32[]{:S(2)}) async-start(), calls=%async_computation.7 | async-start | bytes 28180480 | tf_op jit(solution)/shard_map/all_gather | solution.py:65
  12.9 0.7 copy-start.9
  12.9 0.8 copy-start.4
  12.9 1.2 copy-start
  12.9 3.6 copy-start.2
  12.9 284.1 %all-gather.6.cloned.1.call-start = ((), (), s32[]{:S(2)}) async-start(), calls=%async_computation.3 | async-start | bytes 7077888 | tf_op jit(solution)/shard_map/all_gather | solution.py:59
  15.2 385.5 %all-gather.8.cloned.1.call-start = ((), (), s32[]{:S(2)}) async-start(), calls=%async_computation.4 | async-start | bytes 14090240 | tf_op jit(solution)/shard_map/all_gather | solution.py:70
  15.9 498.0 %all-gather.10.cloned.1.call-start = ((), (), s32[]{:S(2)}) async-start(), calls=%async_computation.5 | async-start | bytes 14090240 | tf_op jit(solution)/shard_map/all_gather | solution.py:71
  16.5 569.3 %reduce-scatter.3.cloned.1.call-start = ((), (), s32[]{:S(2)}) async-start(), calls=%async_computation.2 | async-start | bytes 7077888 | tf_op jit(solution)/shard_map/reduce_scatter | solution.py:73
  251.0 12.8 %copy-start.6 = (bf16[768,1376]{0,1:T(8,128)(2,1)S(1)}, bf16[768,1376]{0,1:T(8,128)(2,1)}, u32[]{:S(2)}) copy-start(bf16[768,1376]{0,1:T(8,128)(2,1)} %param.15) | copy-start | bytes 6340612
  296.3 0.7 copy-start.3
  296.4 2.1 copy-start.7
  296.4 491.4 %reduce-scatter.5.cloned.1.call-start = ((), (), s32[]{:S(2)}) async-start(), calls=%async_computation.6 | async-start | bytes 28180480 | tf_op jit(solution)/shard_map/reduce_scatter | solution.py:85
  298.5 16.4 %copy-start.5 = (bf16[768,4096]{1,0:T(8,128)(2,1)S(1)}, bf16[768,4096]{1,0:T(8,128)(2,1)}, u32[]{:S(2)}) copy-start(bf16[768,4096]{1,0:T(8,128)(2,1)} %all-gather.6.cloned.1.call-done) | copy-start | bytes 18874372
  298.5 16.4 %copy-start.8 = (bf16[768,1376]{0,1:T(8,128)(2,1)S(1)}, bf16[768,1376]{0,1:T(8,128)(2,1)}, u32[]{:S(2)}) copy-start(bf16[768,1376]{0,1:T(8,128)(2,1)} %param.21) | copy-start | bytes 6340612
  415.8 170.1 %copy-start.1 = (bf16[768,512]{1,0:T(8,128)(2,1)S(1)}, bf16[768,512]{1,0:T(8,128)(2,1)}, u32[]{:S(2)}) copy-start(bf16[768,512]{1,0:T(8,128)(2,1)} %param.16) | copy-start | bytes 2359300
Sparse Core Ops, SparseCore 0:
  13.0 208.7 all-gather.11
  224.0 64.6 all-gather.5
  290.5 110.1 all-gather.7
  402.4 111.4 all-gather.9
  516.0 69.7 reduce-scatter.2
  588.8 198.9 reduce-scatter.4
